TPU v7x, 256 devices: a whole 4x4x8 slice. The times are simulated.
256 devices in a mesh: slab: 256 (over x, z, y, core).
Axes of the slice: x: 4, y: 4, z: 8, core: 2. Of those that a mesh axis runs over, the one named last changes fastest.
Arguments:
- coords: float32 [3, 524288], P(None, 'slab'), may hold values from -18 to 2048, as said below
- charges: float32 [524288], P('slab'), may hold values from -3.6 to 3.6
- radii: float32 [524288], P('slab'), may hold values from 1.2 to 2
- screens: float32 [524288], P('slab'), may hold values from 0.6 to 0.9
- tile_lists: int32 [4096, 8], P('slab'), may hold values from 0 to 79, as said below
- tile_counts: int32 [4096], P('slab'), may hold values from 1 to 8, as said below
- slab_fill: int32 [256], P('slab'), may hold values from 1921 to 2048
Outputs:
- born_radii: float32 [524288], P('slab')
- energy: float32 [524288], P('slab')
- total: float32 [], replicated
Inputs may be any that keep to these rules, and one draw needn't show every extreme that they name: `coords`: x and y lie within 18 of the fibre axis; z of atoms of slab s lies in [8 s, 8 s + 8]. `tile_lists`: entry 0 of tile g's list is its own tile, 32 + g % 16; the entries of a row are distinct; listed tiles lie in slabs that exist (the fibre does not close) and within 32 window tiles of the own tile. `tile_counts`: every slab has a tile whose count is 8.
All inputs are finite; a program needn't handle non-finite values.
Results may differ from a plain program's by a relative error of at most 0.0003.
Values sent between devices are 32-bit elements; how exact they have to be, the bound alone decides.
No kernel may reach another device: no remote copies, remote signals or barrier semaphores. Data moves between devices by JAX's collectives and lax.ppermute only.
A program may use at most 64 MiB of HBM per device.

v0:
```python
import jax
import jax.numpy as jnp
from jax import lax
from jax.sharding import Mesh
from jax.sharding import PartitionSpec as P

SLAB = ("slab_0", "slab_1", "slab_2", "slab_3")
OFFSET = 0.09
SOFTEN = 1.0
group_tiles = 4


def passed_along(value, axis, steps):
    count = lax.axis_size(axis)
    pairs = [(source, (source + steps) % count) for source in range(count)]
    return lax.ppermute(value, axis, pairs)


def by_axis(shard, axes):
    for axis in axes:
        shard = lax.psum(shard, axis)
    return shard


def pair_geometry(own_atoms, partner_atoms, list_block, count_block, first_block):
    squared = jnp.zeros((own_atoms.shape[1], 128, partner_atoms.shape[2], 128), jnp.float32)
    for component in range(3):
        offsets = own_atoms[component][:, :, None, None] - partner_atoms[component][:, None, :, :]
        squared = squared + offsets * offsets
    slot_ids = jnp.arange(partner_atoms.shape[2], dtype=jnp.int32)
    used_slot = (slot_ids[None, :] < count_block[:, None])[:, None, :, None]
    partner_mask = (
        used_slot & (partner_atoms[6] > 0.5)[:, None, :, :] & (own_atoms[6] > 0.5)[:, :, None, None]
    )
    lanes = jnp.arange(128, dtype=jnp.int32)
    own_ids = first_block[:, None] * 128 + lanes[None, :]
    partner_ids = list_block[:, :, None] * 128 + lanes[None, None, :]
    distinct = own_ids[:, :, None, None] != partner_ids[:, None, :, :]
    return (squared, partner_mask, distinct)


def born_block(own_atoms, partner_atoms, list_block, count_block, first_block):
    squared, partner_mask, distinct = pair_geometry(
        own_atoms, partner_atoms, list_block, count_block, first_block
    )
    own_live = own_atoms[6] > 0.5
    radius_own = jnp.where(own_live, own_atoms[4], 1.5)
    radius_partner = jnp.where(partner_atoms[6] > 0.5, partner_atoms[4], 1.5)[:, None, :, :]
    screen_partner = jnp.where(partner_atoms[6] > 0.5, partner_atoms[5], 0.8)[:, None, :, :]
    offset_radius = (radius_own - OFFSET)[:, :, None, None]
    scaled_radius = screen_partner * (radius_partner - OFFSET)
    distance = jnp.sqrt(squared + SOFTEN)
    upper_end = distance + scaled_radius
    lower_end = jnp.maximum(offset_radius, jnp.abs(distance - scaled_radius))
    pair_term = 0.5 * (
        1.0 / lower_end
        - 1.0 / upper_end
        + 0.25
        * (distance - scaled_radius * scaled_radius / distance)
        * (1.0 / (upper_end * upper_end) - 1.0 / (lower_end * lower_end))
        + 0.5 * jnp.log(lower_end / upper_end) / distance
    )
    pair_term = pair_term + jnp.where(
        offset_radius < scaled_radius - distance, 2.0 * (1.0 / offset_radius - 1.0 / lower_end), 0.0
    )
    counted = partner_mask & distinct & (offset_radius < upper_end)
    integral = jnp.sum(jnp.where(counted, pair_term, 0.0), axis=(2, 3))
    inner_radius = radius_own - OFFSET
    psi_value = integral * inner_radius
    bending = jnp.tanh(
        psi_value - 0.8 * psi_value * psi_value + 4.85 * psi_value * psi_value * psi_value
    )
    result = 1.0 / (1.0 / inner_radius - bending / radius_own)
    return jnp.where(own_live, result, 0.0)


def energy_block(
    own_atoms, partner_atoms, radius_own, radius_partner, list_block, count_block, first_block
):
    squared, partner_mask, distinct = pair_geometry(
        own_atoms, partner_atoms, list_block, count_block, first_block
    )
    own_live = own_atoms[6] > 0.5
    born_own = jnp.where(own_live, radius_own, 1.0)[:, :, None, None]
    born_partner = jnp.where(partner_atoms[6] > 0.5, radius_partner, 1.0)[:, None, :, :]
    product = born_own * born_partner
    screened = jnp.sqrt(squared + product * jnp.exp(-squared / (4.0 * product)))
    pair_term = jnp.where(partner_mask, partner_atoms[3][:, None, :, :] / screened, 0.0)
    result = -0.5 * own_atoms[3] * jnp.sum(pair_term, axis=(2, 3))
    return jnp.where(own_live, result, 0.0)


def tile_setup(window, lists, counts):
    width = window.shape[1]
    tiles = width // 640
    blocks = tiles // group_tiles
    tiled = window.reshape(window.shape[0], width // 128, 128)
    own_atoms = (
        tiled[:, 2 * tiles : 3 * tiles]
        .reshape(window.shape[0], blocks, group_tiles, 128)
        .transpose(1, 0, 2, 3)
    )
    list_groups = lists.reshape(blocks, group_tiles, lists.shape[1])
    count_groups = counts.reshape(blocks, group_tiles)
    first_tiles = (2 * tiles + jnp.arange(tiles, dtype=jnp.int32)).reshape(blocks, group_tiles)
    return (tiled, own_atoms, list_groups, count_groups, first_tiles)


def slab_born(window, lists, counts):
    tiled, own_atoms, list_groups, count_groups, first_tiles = tile_setup(window, lists, counts)

    def one_block(inputs):
        own_block, list_block, count_block, first_block = inputs
        partner_atoms = jnp.take(tiled, list_block, axis=1)
        return born_block(own_block, partner_atoms, list_block, count_block, first_block)

    result = lax.map(one_block, (own_atoms, list_groups, count_groups, first_tiles))
    return result.reshape(-1)


def slab_energy(window, radius_window, lists, counts):
    tiled, own_atoms, list_groups, count_groups, first_tiles = tile_setup(window, lists, counts)
    radius_tiled = radius_window.reshape(-1, 128)
    tiles = radius_tiled.shape[0] // 5
    radius_groups = radius_tiled[2 * tiles : 3 * tiles].reshape(-1, group_tiles, 128)

    def one_block(inputs):
        own_block, radius_block, list_block, count_block, first_block = inputs
        partner_atoms = jnp.take(tiled, list_block, axis=1)
        partner_radii = jnp.take(radius_tiled, list_block, axis=0)
        return energy_block(
            own_block,
            partner_atoms,
            radius_block,
            partner_radii,
            list_block,
            count_block,
            first_block,
        )

    result = lax.map(one_block, (own_atoms, radius_groups, list_groups, count_groups, first_tiles))
    return result.reshape(-1)


def window_of(values):
    nearby = [passed_along(values, SLAB, shift_by) for shift_by in (1, -1)]
    distant = [passed_along(values, SLAB, shift_by) for shift_by in (2, -2)]
    return jnp.concatenate([distant[0], nearby[0], values, nearby[1], distant[1]], axis=-1)


def shards(coords, charges, radii, screens, tile_lists, tile_counts, slab_fill):
    atom_count = coords.shape[1]
    live_flag = (jnp.arange(atom_count, dtype=jnp.int32) < slab_fill[0]).astype(jnp.float32)
    packed = jnp.concatenate(
        [coords, charges[None], radii[None], screens[None], live_flag[None]], axis=0
    )
    window = window_of(packed)
    born_radii = slab_born(window, tile_lists, tile_counts)
    radius_window = window_of(born_radii)
    energy = slab_energy(window, radius_window, tile_lists, tile_counts)
    total = by_axis(jnp.sum(energy), SLAB)
    return (born_radii, energy, total)


def solution(mesh):
    torus = Mesh(mesh.devices.reshape(4, 8, 4, 2), ("slab_0", "slab_1", "slab_2", "slab_3"))
    placed = (P(None, SLAB), P(SLAB), P(SLAB), P(SLAB), P(SLAB, None), P(SLAB), P(SLAB))
    return jax.shard_map(
        shards, mesh=torus, in_specs=placed, out_specs=(P(SLAB), P(SLAB), P()), check_vma=False
    )
```

profile of v0, /device:TPU:1, one launch (start us, length us, event | category | flops | bytes accessed | tf_op | source)
XLA Modules:
  0.0 163.9 jit_solution(10497928802857674621)
XLA Ops:
  1.3 0.8 concatenate.21
  2.1 2.2 %collective-permute-start = (f32[7,2048]{1,0:T(8,128)S(1)}, f32[7,2048]{1,0:T(8,128)S(1)}, u32[]{:S(2)}, u32[]{:S(2)}) collective-permute-start(f32[7,2048]{1,0:T(8,128)S(1)} %concatenate.21), channel_id=1, source_target_pairs={{0,2},{1,3},{2,4},{3,5},{4,6},{5,7},{6,8},{7,9},{8,10},{9,11},{10,... | collective-permute-start | bytes 172040 | tf_op jit(solution)/shard_map/ppermute | solution.py:16
  4.3 2.1 %collective-permute-start.1 = (f32[7,2048]{1,0:T(8,128)S(1)}, f32[7,2048]{1,0:T(8,128)S(1)}, u32[]{:S(2)}, u32[]{:S(2)}) collective-permute-start(f32[7,2048]{1,0:T(8,128)S(1)} %concatenate.21), channel_id=1, source_target_pairs={{0,1},{1,2},{2,3},{3,4},{4,5},{5,6},{6,7},{7,8},{8,9},{9,10},{10,1... | collective-permute-start | bytes 172040 | tf_op jit(solution)/shard_map/ppermute | solution.py:16
  6.5 7.6 %collective-permute-start.3 = (f32[7,2048]{1,0:T(8,128)S(1)}, f32[7,2048]{1,0:T(8,128)S(1)}, u32[]{:S(2)}, u32[]{:S(2)}) collective-permute-start(f32[7,2048]{1,0:T(8,128)S(1)} %concatenate.21), channel_id=1, source_target_pairs={{0,254},{1,255},{2,0},{3,1},{4,2},{5,3},{6,4},{7,5},{8,6},{9,7},{1... | collective-permute-start | bytes 172040 | tf_op jit(solution)/shard_map/ppermute | solution.py:16
  14.1 0.8 copy.25
  14.9 0.7 reshape.487
  16.1 47.0 %while.23 = (s32[]{:T(128)}, f32[4,4,128]{2,1,0:T(4,128)S(1)}, f32[4,7,4,128]{3,2,1,0:T(4,128)S(1)}, s32[4,4]{1,0:T(4,128)S(1)}, s32[4,4,8]{2,1,0:T(4,128)S(1)},...) while((s32[]{:T(128)}, f32[4,4,128]{2,1,0:T(4,128)S(1)}, ...), condition=%wide.region_2.4_spmd, body=%wide.region_0.3_spmd.sunk | while | flops 23141128 | bytes 918585 | solution.py:117
  16.2 0.6 gather_fusion
  17.4 10.4 %fusion.63 = f32[4,128]{1,0:T(4,128)S(1)} fusion(f32[4,128]{1,0:T(4,128)S(1)} %get-tuple-element.337, f32[4,8,128]{2,1,0:T(8,128)S(1)} %get-tuple-element.345, f32[4,8,128]{2,1,0:T(8,128)S(1)} %get-tuple-element.346, f32[4,8,128]{2,1,0:T(8,128)S(1)} %bitcast.188, f32[4,128]{1,0:T(4,128)S(1)} %get-tuple-element.348, f32[4,8,128]{2,1,0:T(8,128)S(1)} %bitcast.189, ...), kind=kLoop, calls=%fused_computation.16.clone.1 | loop fusion | flops 23068160 | bytes 117248 | tf_op jit(solution)/shard_map/while/body/eval_jaxpr/reduce_sum | solution.py:67
  28.0 0.6 gather_fusion
  29.1 10.4 %fusion.63 = f32[4,128]{1,0:T(4,128)S(1)} fusion(f32[4,128]{1,0:T(4,128)S(1)} %get-tuple-element.337, f32[4,8,128]{2,1,0:T(8,128)S(1)} %get-tuple-element.345, f32[4,8,128]{2,1,0:T(8,128)S(1)} %get-tuple-element.346, f32[4,8,128]{2,1,0:T(8,128)S(1)} %bitcast.188, f32[4,128]{1,0:T(4,128)S(1)} %get-tuple-element.348, f32[4,8,128]{2,1,0:T(8,128)S(1)} %bitcast.189, ...), kind=kLoop, calls=%fused_computation.16.clone.1 | loop fusion | flops 23068160 | bytes 117248 | tf_op jit(solution)/shard_map/while/body/eval_jaxpr/reduce_sum | solution.py:67
  39.7 0.6 gather_fusion
  40.9 10.4 %fusion.63 = f32[4,128]{1,0:T(4,128)S(1)} fusion(f32[4,128]{1,0:T(4,128)S(1)} %get-tuple-element.337, f32[4,8,128]{2,1,0:T(8,128)S(1)} %get-tuple-element.345, f32[4,8,128]{2,1,0:T(8,128)S(1)} %get-tuple-element.346, f32[4,8,128]{2,1,0:T(8,128)S(1)} %bitcast.188, f32[4,128]{1,0:T(4,128)S(1)} %get-tuple-element.348, f32[4,8,128]{2,1,0:T(8,128)S(1)} %bitcast.189, ...), kind=kLoop, calls=%fused_computation.16.clone.1 | loop fusion | flops 23068160 | bytes 117248 | tf_op jit(solution)/shard_map/while/body/eval_jaxpr/reduce_sum | solution.py:67
  51.5 0.6 gather_fusion
  52.6 10.4 %fusion.63 = f32[4,128]{1,0:T(4,128)S(1)} fusion(f32[4,128]{1,0:T(4,128)S(1)} %get-tuple-element.337, f32[4,8,128]{2,1,0:T(8,128)S(1)} %get-tuple-element.345, f32[4,8,128]{2,1,0:T(8,128)S(1)} %get-tuple-element.346, f32[4,8,128]{2,1,0:T(8,128)S(1)} %bitcast.188, f32[4,128]{1,0:T(4,128)S(1)} %get-tuple-element.348, f32[4,8,128]{2,1,0:T(8,128)S(1)} %bitcast.189, ...), kind=kLoop, calls=%fused_computation.16.clone.1 | loop fusion | flops 23068160 | bytes 117248 | tf_op jit(solution)/shard_map/while/body/eval_jaxpr/reduce_sum | solution.py:67
  63.2 1.4 collective-permute-start.5
  64.6 0.8 collective-permute-start.6
  65.4 7.4 %collective-permute-start.7 = (f32[2048]{0:T(1024)S(1)}, f32[2048]{0:T(1024)S(1)}, u32[]{:S(2)}, u32[]{:S(2)}) collective-permute-start(f32[2048]{0:T(1024)S(1)} %bitcast.195), channel_id=1, source_target_pairs={{0,254},{1,255},{2,0},{3,1},{4,2},{5,3},{6,4},{7,5},{8,6},{9,7},{1... | collective-permute-start | bytes 24584 | tf_op jit(solution)/shard_map/ppermute | solution.py:16
  72.8 0.7 collective-permute-done.7
  73.6 44.1 %while.24 = (s32[]{:T(128)}, f32[4,4,128]{2,1,0:T(4,128)S(1)}, f32[4,7,4,128]{3,2,1,0:T(4,128)S(1)}, s32[4,4]{1,0:T(4,128)S(1)}, s32[4,4,8]{2,1,0:T(4,128)S(1)},...) while((s32[]{:T(128)}, f32[4,4,128]{2,1,0:T(4,128)S(1)}, ...), condition=%wide.region_5.7_spmd, body=%wide.region_3.6_spmd.sunk | while | flops 9486662 | bytes 816557 | solution.py:141
  73.7 0.6 gather_fusion.1
  75.3 9.3 %select_reduce_fusion.2 = f32[4,128]{1,0:T(4,128)S(1)} fusion(f32[4,8,128]{2,1,0:T(8,128)S(1)} %fusion.66, f32[4,128]{1,0:T(4,128)S(1)} %get-tuple-element.368, f32[4,8,128]{2,1,0:T(8,128)S(1)} %get-tuple-element.369, f32[4,128]{1,0:T(4,128)S(1)} %get-tuple-element.370, f32[4,8,128]{2,1,0:T(8,128)S(1)} %get-tuple-element.371, ...), kind=kLoop, calls=%fused_computation.63.clone.1 | loop fusion | flops 9436672 | bytes 96768 | tf_op jit(solution)/shard_map/while/body/eval_jaxpr/reduce_sum | solution.py:89
  84.7 0.6 gather_fusion.1
  86.4 9.3 %select_reduce_fusion.2 = f32[4,128]{1,0:T(4,128)S(1)} fusion(f32[4,8,128]{2,1,0:T(8,128)S(1)} %fusion.66, f32[4,128]{1,0:T(4,128)S(1)} %get-tuple-element.368, f32[4,8,128]{2,1,0:T(8,128)S(1)} %get-tuple-element.369, f32[4,128]{1,0:T(4,128)S(1)} %get-tuple-element.370, f32[4,8,128]{2,1,0:T(8,128)S(1)} %get-tuple-element.371, ...), kind=kLoop, calls=%fused_computation.63.clone.1 | loop fusion | flops 9436672 | bytes 96768 | tf_op jit(solution)/shard_map/while/body/eval_jaxpr/reduce_sum | solution.py:89
  95.8 0.6 gather_fusion.1
  97.4 9.3 %select_reduce_fusion.2 = f32[4,128]{1,0:T(4,128)S(1)} fusion(f32[4,8,128]{2,1,0:T(8,128)S(1)} %fusion.66, f32[4,128]{1,0:T(4,128)S(1)} %get-tuple-element.368, f32[4,8,128]{2,1,0:T(8,128)S(1)} %get-tuple-element.369, f32[4,128]{1,0:T(4,128)S(1)} %get-tuple-element.370, f32[4,8,128]{2,1,0:T(8,128)S(1)} %get-tuple-element.371, ...), kind=kLoop, calls=%fused_computation.63.clone.1 | loop fusion | flops 9436672 | bytes 96768 | tf_op jit(solution)/shard_map/while/body/eval_jaxpr/reduce_sum | solution.py:89
  108.4 9.3 %select_reduce_fusion.2 = f32[4,128]{1,0:T(4,128)S(1)} fusion(f32[4,8,128]{2,1,0:T(8,128)S(1)} %fusion.66, f32[4,128]{1,0:T(4,128)S(1)} %get-tuple-element.368, f32[4,8,128]{2,1,0:T(8,128)S(1)} %get-tuple-element.369, f32[4,128]{1,0:T(4,128)S(1)} %get-tuple-element.370, f32[4,8,128]{2,1,0:T(8,128)S(1)} %get-tuple-element.371, ...), kind=kLoop, calls=%fused_computation.63.clone.1 | loop fusion | flops 9436672 | bytes 96768 | tf_op jit(solution)/shard_map/while/body/eval_jaxpr/reduce_sum | solution.py:89
  117.7 0.6 reduce_sum.35
  118.3 6.6 %psum.28 = f32[]{:T(128)} all-reduce(f32[]{:T(128)} %reduce_sum.35), channel_id=1, replica_groups=mesh['slab_0'=4,'slab_1'=8,'slab_2'=4,'slab_3'=2] {'slab_0'}, use_global_device_ids=true, to_apply=%region_7.9 | all-reduce | flops 1 | bytes 8 | tf_op jit(solution)/shard_map/psum | solution.py:21
  124.9 12.9 %psum.29 = f32[]{:T(128)} all-reduce(f32[]{:T(128)} %psum.28), channel_id=1, replica_groups=mesh['slab_0'=4,'slab_1'=8,'slab_2'=4,'slab_3'=2] {'slab_1'}, use_global_device_ids=true, to_apply=%region_8.10 | all-reduce | flops 1 | bytes 8 | tf_op jit(solution)/shard_map/psum | solution.py:21
  137.9 12.6 %psum.30 = f32[]{:T(128)} all-reduce(f32[]{:T(128)} %psum.29), channel_id=1, replica_groups=mesh['slab_0'=4,'slab_1'=8,'slab_2'=4,'slab_3'=2] {'slab_2'}, use_global_device_ids=true, to_apply=%region_9.11 | all-reduce | flops 1 | bytes 8 | tf_op jit(solution)/shard_map/psum | solution.py:21
  150.5 13.3 %psum.31 = f32[]{:T(128)} all-reduce(f32[]{:T(128)} %psum.30), channel_id=1, replica_groups=mesh['slab_0'=4,'slab_1'=8,'slab_2'=4,'slab_3'=2] {'slab_3'}, use_global_device_ids=true, to_apply=%region_10.12 | all-reduce | flops 1 | bytes 8 | tf_op jit(solution)/shard_map/psum | solution.py:21
  (154 shorter events, 8.3 us)
Async XLA Ops:
  2.1 13.5 %collective-permute-start = (f32[7,2048]{1,0:T(8,128)S(1)}, f32[7,2048]{1,0:T(8,128)S(1)}, u32[]{:S(2)}, u32[]{:S(2)}) collective-permute-start(f32[7,2048]{1,0:T(8,128)S(1)} %concatenate.21), channel_id=1, source_target_pairs={{0,2},{1,3},{2,4},{3,5},{4,6},{5,7},{6,8},{7,9},{8,10},{9,11},{10,... | collective-permute-start | bytes 172040 | tf_op jit(solution)/shard_map/ppermute | solution.py:16
  4.3 11.3 %collective-permute-start.1 = (f32[7,2048]{1,0:T(8,128)S(1)}, f32[7,2048]{1,0:T(8,128)S(1)}, u32[]{:S(2)}, u32[]{:S(2)}) collective-permute-start(f32[7,2048]{1,0:T(8,128)S(1)} %concatenate.21), channel_id=1, source_target_pairs={{0,1},{1,2},{2,3},{3,4},{4,5},{5,6},{6,7},{7,8},{8,9},{9,10},{10,1... | collective-permute-start | bytes 172040 | tf_op jit(solution)/shard_map/ppermute | solution.py:16
  6.5 9.2 %collective-permute-start.2 = (f32[7,2048]{1,0:T(8,128)S(1)}, f32[7,2048]{1,0:T(8,128)S(1)}, u32[]{:S(2)}, u32[]{:S(2)}) collective-permute-start(f32[7,2048]{1,0:T(8,128)S(1)} %concatenate.21), channel_id=1, source_target_pairs={{0,255},{1,0},{2,1},{3,2},{4,3},{5,4},{6,5},{7,6},{8,7},{9,8},{10,... | collective-permute-start | bytes 172040 | tf_op jit(solution)/shard_map/ppermute | solution.py:16
  6.5 9.5 %collective-permute-start.3 = (f32[7,2048]{1,0:T(8,128)S(1)}, f32[7,2048]{1,0:T(8,128)S(1)}, u32[]{:S(2)}, u32[]{:S(2)}) collective-permute-start(f32[7,2048]{1,0:T(8,128)S(1)} %concatenate.21), channel_id=1, source_target_pairs={{0,254},{1,255},{2,0},{3,1},{4,2},{5,3},{6,4},{7,5},{8,6},{9,7},{1... | collective-permute-start | bytes 172040 | tf_op jit(solution)/shard_map/ppermute | solution.py:16
  63.1 9.7 %collective-permute-start.4 = (f32[2048]{0:T(1024)S(1)}, f32[2048]{0:T(1024)S(1)}, u32[]{:S(2)}, u32[]{:S(2)}) collective-permute-start(f32[2048]{0:T(1024)S(1)} %bitcast.192), channel_id=1, source_target_pairs={{0,2},{1,3},{2,4},{3,5},{4,6},{5,7},{6,8},{7,9},{8,10},{9,11},{10,... | collective-permute-start | bytes 24584 | tf_op jit(solution)/shard_map/ppermute | solution.py:16
  63.2 9.6 %collective-permute-start.5 = (f32[2048]{0:T(1024)S(1)}, f32[2048]{0:T(1024)S(1)}, u32[]{:S(2)}, u32[]{:S(2)}) collective-permute-start(f32[2048]{0:T(1024)S(1)} %bitcast.193), channel_id=1, source_target_pairs={{0,1},{1,2},{2,3},{3,4},{4,5},{5,6},{6,7},{7,8},{8,9},{9,10},{10,1... | collective-permute-start | bytes 24584 | tf_op jit(solution)/shard_map/ppermute | solution.py:16
  64.6 8.2 %collective-permute-start.6 = (f32[2048]{0:T(1024)S(1)}, f32[2048]{0:T(1024)S(1)}, u32[]{:S(2)}, u32[]{:S(2)}) collective-permute-start(f32[2048]{0:T(1024)S(1)} %bitcast.194), channel_id=1, source_target_pairs={{0,255},{1,0},{2,1},{3,2},{4,3},{5,4},{6,5},{7,6},{8,7},{9,8},{10,... | collective-permute-start | bytes 24584 | tf_op jit(solution)/shard_map/ppermute | solution.py:16
  65.4 8.2 %collective-permute-start.7 = (f32[2048]{0:T(1024)S(1)}, f32[2048]{0:T(1024)S(1)}, u32[]{:S(2)}, u32[]{:S(2)}) collective-permute-start(f32[2048]{0:T(1024)S(1)} %bitcast.195), channel_id=1, source_target_pairs={{0,254},{1,255},{2,0},{3,1},{4,2},{5,3},{6,4},{7,5},{8,6},{9,7},{1... | collective-permute-start | bytes 24584 | tf_op jit(solution)/shard_map/ppermute | solution.py:16
  117.7 46.2 %copy-start = (f32[4,4,128]{2,1,0:T(4,128)}, f32[4,4,128]{2,1,0:T(4,128)S(1)}, u32[]{:S(2)}) copy-start(f32[4,4,128]{2,1,0:T(4,128)S(1)} %get-tuple-element.470) | copy-start | bytes 24580
  117.7 46.1 %copy-start.1 = (f32[4,4,128]{2,1,0:T(4,128)}, f32[4,4,128]{2,1,0:T(4,128)S(1)}, u32[]{:S(2)}) copy-start(f32[4,4,128]{2,1,0:T(4,128)S(1)} %get-tuple-element.156) | copy-start | bytes 24580
where the time goes:
time: 164 us
  other arithmetic  82.8 us (50%)
  blocking collectives  45.5 us (28%)
  starting transfers between devices  21.7 us (13%)
  local copies, waits for them, and re-layouts  10.9 us (7%)
    psum x4, blocking collectives, by_axis(): shard = lax.psum(shard, axis)  45.5 us
    reduce_sum x4, other arithmetic, born_block(): integral = jnp.sum(jnp.where(counted, pair_term, 0.0), axis=(2, 3))  41.8 us
    reduce_sum x4, other arithmetic, energy_block(): result = -0.5 * own_atoms[3] * jnp.sum(pair_term, axis=(2, 3))  37 us
    ppermute x8, starting transfers between devices, passed_along(): return lax.ppermute(value, axis, pairs)  21.7 us
    gather x8, local copies, waits for them, and re-layouts, one_block(): partner_atoms = jnp.take(tiled, list_block, axis=1)  4.68 us
  transfers between devices with their start and end apart: 8, of which 2 were waited for; matrix products, arithmetic and copies ran while one was open for 1% of the time, Pallas kernels for 0%

commit v1 on v0

--- a/solution.py
+++ b/solution.py
@@ -18,7 +18,7 @@
 
 def by_axis(shard, axes):
     for axis in axes:
-        shard = lax.psum(shard, axis)
+        shard = jnp.sum(lax.all_gather(shard, axis), axis=0)
     return shard
 
 

time: 164 us -> 173 us (1.055)
  local copies, waits for them, and re-layouts: 10.9 us -> 19.3 us
  other arithmetic: 82.8 us -> 85.2 us
  blocking collectives: 45.5 us -> 43.1 us
    psum x4 -> x0, blocking collectives: 45.5 us -> none  [by_axis(): shard = lax.psum(shard, axis)]
    unnamed x0 -> x4, blocking collectives: none -> 43.1 us
    unnamed x13 -> x33, local copies, waits for them, and re-layouts: 0.81 us -> 9.26 us
    reduce_sum x0 -> x4, other arithmetic: none -> 2.41 us  [by_axis(): shard = jnp.sum(lax.all_gather(shard, axis), axis=0)]
where the time goes in v1:
time: 173 us; the launch traced here: 172 us
  other arithmetic  85.2 us (49%)
  blocking collectives  43.1 us (25%)
  starting transfers between devices  21.5 us (12%)
  local copies, waits for them, and re-layouts  19.3 us (11%)
    unnamed x4, blocking collectives  43.1 us
    reduce_sum x4, other arithmetic, born_block(): integral = jnp.sum(jnp.where(counted, pair_term, 0.0), axis=(2, 3))  41.8 us
    reduce_sum x4, other arithmetic, energy_block(): result = -0.5 * own_atoms[3] * jnp.sum(pair_term, axis=(2, 3))  37 us
    ppermute x8, starting transfers between devices, passed_along(): return lax.ppermute(value, axis, pairs)  21.5 us
    unnamed x33, local copies, waits for them, and re-layouts  9.26 us
    gather x8, local copies, waits for them, and re-layouts, one_block(): partner_atoms = jnp.take(tiled, list_block, axis=1)  4.68 us
  transfers between devices with their start and end apart: 8, of which 2 were waited for; matrix products, arithmetic and copies ran while one was open for 1% of the time, Pallas kernels for 0%

profile of v1, /device:TPU:1, one launch (start us, length us, event | category | flops | bytes accessed | tf_op | source)
XLA Modules:
  0.0 172.2 jit_solution(17859064888641332485)
XLA Ops:
  1.3 0.8 concatenate.21
  2.1 2.2 %collective-permute-start = (f32[7,2048]{1,0:T(8,128)S(1)}, f32[7,2048]{1,0:T(8,128)S(1)}, u32[]{:S(2)}, u32[]{:S(2)}) collective-permute-start(f32[7,2048]{1,0:T(8,128)S(1)} %concatenate.21), channel_id=1, source_target_pairs={{0,2},{1,3},{2,4},{3,5},{4,6},{5,7},{6,8},{7,9},{8,10},{9,11},{10,... | collective-permute-start | bytes 172040 | tf_op jit(solution)/shard_map/ppermute | solution.py:16
  4.3 2.1 %collective-permute-start.1 = (f32[7,2048]{1,0:T(8,128)S(1)}, f32[7,2048]{1,0:T(8,128)S(1)}, u32[]{:S(2)}, u32[]{:S(2)}) collective-permute-start(f32[7,2048]{1,0:T(8,128)S(1)} %concatenate.21), channel_id=1, source_target_pairs={{0,1},{1,2},{2,3},{3,4},{4,5},{5,6},{6,7},{7,8},{8,9},{9,10},{10,1... | collective-permute-start | bytes 172040 | tf_op jit(solution)/shard_map/ppermute | solution.py:16
  6.5 7.6 %collective-permute-start.3 = (f32[7,2048]{1,0:T(8,128)S(1)}, f32[7,2048]{1,0:T(8,128)S(1)}, u32[]{:S(2)}, u32[]{:S(2)}) collective-permute-start(f32[7,2048]{1,0:T(8,128)S(1)} %concatenate.21), channel_id=1, source_target_pairs={{0,254},{1,255},{2,0},{3,1},{4,2},{5,3},{6,4},{7,5},{8,6},{9,7},{1... | collective-permute-start | bytes 172040 | tf_op jit(solution)/shard_map/ppermute | solution.py:16
  14.1 0.8 copy.25
  14.9 0.7 reshape.487
  16.1 47.0 %while.23 = (s32[]{:T(128)}, f32[4,4,128]{2,1,0:T(4,128)S(1)}, f32[4,7,4,128]{3,2,1,0:T(4,128)S(1)}, s32[4,4]{1,0:T(4,128)S(1)}, s32[4,4,8]{2,1,0:T(4,128)S(1)},...) while((s32[]{:T(128)}, f32[4,4,128]{2,1,0:T(4,128)S(1)}, ...), condition=%wide.region_2.4_spmd, body=%wide.region_0.3_spmd.sunk | while | flops 23141128 | bytes 918585 | solution.py:117
  17.4 10.4 %fusion.63 = f32[4,128]{1,0:T(4,128)S(1)} fusion(f32[4,128]{1,0:T(4,128)S(1)} %get-tuple-element.337, f32[4,8,128]{2,1,0:T(8,128)S(1)} %get-tuple-element.345, f32[4,8,128]{2,1,0:T(8,128)S(1)} %get-tuple-element.346, f32[4,8,128]{2,1,0:T(8,128)S(1)} %bitcast.196, f32[4,128]{1,0:T(4,128)S(1)} %get-tuple-element.348, f32[4,8,128]{2,1,0:T(8,128)S(1)} %bitcast.197, ...), kind=kLoop, calls=%fused_computation.16.clone.1 | loop fusion | flops 23068160 | bytes 117248 | tf_op jit(solution)/shard_map/while/body/eval_jaxpr/reduce_sum | solution.py:67
  29.1 10.4 %fusion.63 = f32[4,128]{1,0:T(4,128)S(1)} fusion(f32[4,128]{1,0:T(4,128)S(1)} %get-tuple-element.337, f32[4,8,128]{2,1,0:T(8,128)S(1)} %get-tuple-element.345, f32[4,8,128]{2,1,0:T(8,128)S(1)} %get-tuple-element.346, f32[4,8,128]{2,1,0:T(8,128)S(1)} %bitcast.196, f32[4,128]{1,0:T(4,128)S(1)} %get-tuple-element.348, f32[4,8,128]{2,1,0:T(8,128)S(1)} %bitcast.197, ...), kind=kLoop, calls=%fused_computation.16.clone.1 | loop fusion | flops 23068160 | bytes 117248 | tf_op jit(solution)/shard_map/while/body/eval_jaxpr/reduce_sum | solution.py:67
  40.9 10.4 %fusion.63 = f32[4,128]{1,0:T(4,128)S(1)} fusion(f32[4,128]{1,0:T(4,128)S(1)} %get-tuple-element.337, f32[4,8,128]{2,1,0:T(8,128)S(1)} %get-tuple-element.345, f32[4,8,128]{2,1,0:T(8,128)S(1)} %get-tuple-element.346, f32[4,8,128]{2,1,0:T(8,128)S(1)} %bitcast.196, f32[4,128]{1,0:T(4,128)S(1)} %get-tuple-element.348, f32[4,8,128]{2,1,0:T(8,128)S(1)} %bitcast.197, ...), kind=kLoop, calls=%fused_computation.16.clone.1 | loop fusion | flops 23068160 | bytes 117248 | tf_op jit(solution)/shard_map/while/body/eval_jaxpr/reduce_sum | solution.py:67
  52.6 10.4 %fusion.63 = f32[4,128]{1,0:T(4,128)S(1)} fusion(f32[4,128]{1,0:T(4,128)S(1)} %get-tuple-element.337, f32[4,8,128]{2,1,0:T(8,128)S(1)} %get-tuple-element.345, f32[4,8,128]{2,1,0:T(8,128)S(1)} %get-tuple-element.346, f32[4,8,128]{2,1,0:T(8,128)S(1)} %bitcast.196, f32[4,128]{1,0:T(4,128)S(1)} %get-tuple-element.348, f32[4,8,128]{2,1,0:T(8,128)S(1)} %bitcast.197, ...), kind=kLoop, calls=%fused_computation.16.clone.1 | loop fusion | flops 23068160 | bytes 117248 | tf_op jit(solution)/shard_map/while/body/eval_jaxpr/reduce_sum | solution.py:67
  63.2 0.7 dynamic-slice
  63.9 1.3 collective-permute-start.5
  65.2 0.7 collective-permute-start.6
  65.9 7.4 %collective-permute-start.7 = (f32[2048]{0:T(1024)S(1)}, f32[2048]{0:T(1024)S(1)}, u32[]{:S(2)}, u32[]{:S(2)}) collective-permute-start(f32[2048]{0:T(1024)S(1)} %bitcast.203), channel_id=1, source_target_pairs={{0,254},{1,255},{2,0},{3,1},{4,2},{5,3},{6,4},{7,5},{8,6},{9,7},{1... | collective-permute-start | bytes 24584 | tf_op jit(solution)/shard_map/ppermute | solution.py:16
  73.4 0.7 collective-permute-done.7
  74.1 44.1 %while.24 = (s32[]{:T(128)}, f32[4,4,128]{2,1,0:T(4,128)S(1)}, f32[4,7,4,128]{3,2,1,0:T(4,128)S(1)}, s32[4,4]{1,0:T(4,128)S(1)}, s32[4,4,8]{2,1,0:T(4,128)S(1)},...) while((s32[]{:T(128)}, f32[4,4,128]{2,1,0:T(4,128)S(1)}, ...), condition=%wide.region_5.7_spmd, body=%wide.region_3.6_spmd.sunk | while | flops 9486662 | bytes 816557 | solution.py:141
  75.9 9.3 %select_reduce_fusion.2 = f32[4,128]{1,0:T(4,128)S(1)} fusion(f32[4,8,128]{2,1,0:T(8,128)S(1)} %fusion.66, f32[4,128]{1,0:T(4,128)S(1)} %get-tuple-element.368, f32[4,8,128]{2,1,0:T(8,128)S(1)} %get-tuple-element.369, f32[4,128]{1,0:T(4,128)S(1)} %get-tuple-element.370, f32[4,8,128]{2,1,0:T(8,128)S(1)} %get-tuple-element.371, ...), kind=kLoop, calls=%fused_computation.63.clone.1 | loop fusion | flops 9436672 | bytes 96768 | tf_op jit(solution)/shard_map/while/body/eval_jaxpr/reduce_sum | solution.py:89
  86.9 9.3 %select_reduce_fusion.2 = f32[4,128]{1,0:T(4,128)S(1)} fusion(f32[4,8,128]{2,1,0:T(8,128)S(1)} %fusion.66, f32[4,128]{1,0:T(4,128)S(1)} %get-tuple-element.368, f32[4,8,128]{2,1,0:T(8,128)S(1)} %get-tuple-element.369, f32[4,128]{1,0:T(4,128)S(1)} %get-tuple-element.370, f32[4,8,128]{2,1,0:T(8,128)S(1)} %get-tuple-element.371, ...), kind=kLoop, calls=%fused_computation.63.clone.1 | loop fusion | flops 9436672 | bytes 96768 | tf_op jit(solution)/shard_map/while/body/eval_jaxpr/reduce_sum | solution.py:89
  98.0 9.3 %select_reduce_fusion.2 = f32[4,128]{1,0:T(4,128)S(1)} fusion(f32[4,8,128]{2,1,0:T(8,128)S(1)} %fusion.66, f32[4,128]{1,0:T(4,128)S(1)} %get-tuple-element.368, f32[4,8,128]{2,1,0:T(8,128)S(1)} %get-tuple-element.369, f32[4,128]{1,0:T(4,128)S(1)} %get-tuple-element.370, f32[4,8,128]{2,1,0:T(8,128)S(1)} %get-tuple-element.371, ...), kind=kLoop, calls=%fused_computation.63.clone.1 | loop fusion | flops 9436672 | bytes 96768 | tf_op jit(solution)/shard_map/while/body/eval_jaxpr/reduce_sum | solution.py:89
  109.0 9.3 %select_reduce_fusion.2 = f32[4,128]{1,0:T(4,128)S(1)} fusion(f32[4,8,128]{2,1,0:T(8,128)S(1)} %fusion.66, f32[4,128]{1,0:T(4,128)S(1)} %get-tuple-element.368, f32[4,8,128]{2,1,0:T(8,128)S(1)} %get-tuple-element.369, f32[4,128]{1,0:T(4,128)S(1)} %get-tuple-element.370, f32[4,8,128]{2,1,0:T(8,128)S(1)} %get-tuple-element.371, ...), kind=kLoop, calls=%fused_computation.63.clone.1 | loop fusion | flops 9436672 | bytes 96768 | tf_op jit(solution)/shard_map/while/body/eval_jaxpr/reduce_sum | solution.py:89
  118.9 1.4 dynamic-update-slice
  120.3 0.7 dynamic-slice.1
  121.0 6.0 %all-reduce = f32[4]{0:T(128)S(1)} all-reduce(f32[4]{0:T(128)S(1)} %dynamic-update-slice), channel_id=1, replica_groups=mesh['slab_0'=4,'slab_1'=8,'slab_2'=4,'slab_3'=2] {'slab_0'}, use_global_device_ids=true, to_apply=%add | all-reduce | flops 4 | bytes 32
  127.6 1.4 dynamic-update-slice.1
  129.0 0.7 dynamic-slice.2
  129.7 12.5 %all-reduce.1 = f32[8]{0:T(128)S(1)} all-reduce(f32[8]{0:T(128)S(1)} %dynamic-update-slice.1), channel_id=1, replica_groups=mesh['slab_0'=4,'slab_1'=8,'slab_2'=4,'slab_3'=2] {'slab_1'}, use_global_device_ids=true, to_apply=%add.1 | all-reduce | flops 8 | bytes 64
  142.8 1.4 dynamic-update-slice.2
  144.2 0.7 dynamic-slice.3
  144.9 11.9 %all-reduce.2 = f32[4]{0:T(128)S(1)} all-reduce(f32[4]{0:T(128)S(1)} %dynamic-update-slice.2), channel_id=1, replica_groups=mesh['slab_0'=4,'slab_1'=8,'slab_2'=4,'slab_3'=2] {'slab_2'}, use_global_device_ids=true, to_apply=%add.2 | all-reduce | flops 4 | bytes 32
  157.4 1.4 dynamic-update-slice.3
  158.9 12.7 %all-reduce.3 = f32[2]{0:T(128)S(1)} all-reduce(f32[2]{0:T(128)S(1)} %dynamic-update-slice.3), channel_id=1, replica_groups=mesh['slab_0'=4,'slab_1'=8,'slab_2'=4,'slab_3'=2] {'slab_3'}, use_global_device_ids=true, to_apply=%add.3 | all-reduce | flops 2 | bytes 16
  (178 shorter events, 15.4 us)
Async XLA Ops:
  2.1 13.5 %collective-permute-start = (f32[7,2048]{1,0:T(8,128)S(1)}, f32[7,2048]{1,0:T(8,128)S(1)}, u32[]{:S(2)}, u32[]{:S(2)}) collective-permute-start(f32[7,2048]{1,0:T(8,128)S(1)} %concatenate.21), channel_id=1, source_target_pairs={{0,2},{1,3},{2,4},{3,5},{4,6},{5,7},{6,8},{7,9},{8,10},{9,11},{10,... | collective-permute-start | bytes 172040 | tf_op jit(solution)/shard_map/ppermute | solution.py:16
  4.3 11.3 %collective-permute-start.1 = (f32[7,2048]{1,0:T(8,128)S(1)}, f32[7,2048]{1,0:T(8,128)S(1)}, u32[]{:S(2)}, u32[]{:S(2)}) collective-permute-start(f32[7,2048]{1,0:T(8,128)S(1)} %concatenate.21), channel_id=1, source_target_pairs={{0,1},{1,2},{2,3},{3,4},{4,5},{5,6},{6,7},{7,8},{8,9},{9,10},{10,1... | collective-permute-start | bytes 172040 | tf_op jit(solution)/shard_map/ppermute | solution.py:16
  6.5 9.2 %collective-permute-start.2 = (f32[7,2048]{1,0:T(8,128)S(1)}, f32[7,2048]{1,0:T(8,128)S(1)}, u32[]{:S(2)}, u32[]{:S(2)}) collective-permute-start(f32[7,2048]{1,0:T(8,128)S(1)} %concatenate.21), channel_id=1, source_target_pairs={{0,255},{1,0},{2,1},{3,2},{4,3},{5,4},{6,5},{7,6},{8,7},{9,8},{10,... | collective-permute-start | bytes 172040 | tf_op jit(solution)/shard_map/ppermute | solution.py:16
  6.5 9.5 %collective-permute-start.3 = (f32[7,2048]{1,0:T(8,128)S(1)}, f32[7,2048]{1,0:T(8,128)S(1)}, u32[]{:S(2)}, u32[]{:S(2)}) collective-permute-start(f32[7,2048]{1,0:T(8,128)S(1)} %concatenate.21), channel_id=1, source_target_pairs={{0,254},{1,255},{2,0},{3,1},{4,2},{5,3},{6,4},{7,5},{8,6},{9,7},{1... | collective-permute-start | bytes 172040 | tf_op jit(solution)/shard_map/ppermute | solution.py:16
  16.1 47.1 %copy-start.5 = (u32[256]{0:T(256)S(1)}, u32[256]{0:T(256)}, u32[]{:S(2)}) copy-start(u32[256]{0:T(256)} %constant.154) | copy-start | bytes 3076
  63.1 10.2 %collective-permute-start.4 = (f32[2048]{0:T(1024)S(1)}, f32[2048]{0:T(1024)S(1)}, u32[]{:S(2)}, u32[]{:S(2)}) collective-permute-start(f32[2048]{0:T(1024)S(1)} %bitcast.200), channel_id=1, source_target_pairs={{0,2},{1,3},{2,4},{3,5},{4,6},{5,7},{6,8},{7,9},{8,10},{9,11},{10,... | collective-permute-start | bytes 24584 | tf_op jit(solution)/shard_map/ppermute | solution.py:16
  63.9 9.5 %collective-permute-start.5 = (f32[2048]{0:T(1024)S(1)}, f32[2048]{0:T(1024)S(1)}, u32[]{:S(2)}, u32[]{:S(2)}) collective-permute-start(f32[2048]{0:T(1024)S(1)} %bitcast.201), channel_id=1, source_target_pairs={{0,1},{1,2},{2,3},{3,4},{4,5},{5,6},{6,7},{7,8},{8,9},{9,10},{10,1... | collective-permute-start | bytes 24584 | tf_op jit(solution)/shard_map/ppermute | solution.py:16
  65.2 8.1 %collective-permute-start.6 = (f32[2048]{0:T(1024)S(1)}, f32[2048]{0:T(1024)S(1)}, u32[]{:S(2)}, u32[]{:S(2)}) collective-permute-start(f32[2048]{0:T(1024)S(1)} %bitcast.202), channel_id=1, source_target_pairs={{0,255},{1,0},{2,1},{3,2},{4,3},{5,4},{6,5},{7,6},{8,7},{9,8},{10,... | collective-permute-start | bytes 24584 | tf_op jit(solution)/shard_map/ppermute | solution.py:16
  65.9 8.2 %collective-permute-start.7 = (f32[2048]{0:T(1024)S(1)}, f32[2048]{0:T(1024)S(1)}, u32[]{:S(2)}, u32[]{:S(2)}) collective-permute-start(f32[2048]{0:T(1024)S(1)} %bitcast.203), channel_id=1, source_target_pairs={{0,254},{1,255},{2,0},{3,1},{4,2},{5,3},{6,4},{7,5},{8,6},{9,7},{1... | collective-permute-start | bytes 24584 | tf_op jit(solution)/shard_map/ppermute | solution.py:16
  74.1 46.2 %copy-start.4 = (u32[256]{0:T(256)S(1)}, u32[256]{0:T(256)}, u32[]{:S(2)}) copy-start(u32[256]{0:T(256)} %constant.159) | copy-start | bytes 3076
  74.1 54.9 %copy-start.3 = (u32[256]{0:T(256)S(1)}, u32[256]{0:T(256)}, u32[]{:S(2)}) copy-start(u32[256]{0:T(256)} %constant.164) | copy-start | bytes 3076
  74.1 70.1 %copy-start.2 = (u32[256]{0:T(256)S(1)}, u32[256]{0:T(256)}, u32[]{:S(2)}) copy-start(u32[256]{0:T(256)} %constant.169) | copy-start | bytes 3076
  118.3 53.9 %copy-start = (f32[4,4,128]{2,1,0:T(4,128)}, f32[4,4,128]{2,1,0:T(4,128)S(1)}, u32[]{:S(2)}) copy-start(f32[4,4,128]{2,1,0:T(4,128)S(1)} %get-tuple-element.470) | copy-start | bytes 24580
  118.3 53.9 %copy-start.1 = (f32[4,4,128]{2,1,0:T(4,128)}, f32[4,4,128]{2,1,0:T(4,128)S(1)}, u32[]{:S(2)}) copy-start(f32[4,4,128]{2,1,0:T(4,128)S(1)} %get-tuple-element.156) | copy-start | bytes 24580
